TPU v7x, 32 devices: a whole 2x2x4 slice. The times are simulated.
32 devices in a mesh: seq: 8 (over z, y), grp: 4 (over x, core).
Axes of the slice: x: 2, y: 2, z: 4, core: 2. Of those that a mesh axis runs over, the one named last changes fastest.
Arguments:
- tokens: bfloat16 [4096, 2560], P('seq'), may hold values from -6 to 6
- norm_gain: float32 [2560], replicated, may hold values from 0.25 to 1.75
- inner_weight: bfloat16 [2560, 2, 5120], P(None, None, ('grp', 'seq')), may hold values from -0.125 to 0.125
- state_weight: bfloat16 [2560, 2, 128], replicated, may hold values from -0.125 to 0.125
- step_weight: bfloat16 [2560, 80], P(None, 'grp'), may hold values from -0.125 to 0.125
- step_bias: float32 [80], P('grp'), may hold values from -1 to 1
- decay_rate: float32 [80], P('grp'), may hold values from 4.8828124e-06 to 0.05
- skip_scale: float32 [80], P('grp'), may hold values from 0.5 to 1.5
- conv_inner: bfloat16 [4, 5120], P(None, 'grp'), may hold values from -3 to 3
- conv_state: bfloat16 [4, 2, 128], replicated, may hold values from -3 to 3
- out_gain: float32 [5120], P('grp'), may hold values from 0.25 to 1.75
- out_weight: bfloat16 [5120, 2560], P(None, 'grp'), may hold values from -0.078125 to 0.078125
Outputs:
- mixed: bfloat16 [4096, 2560], P('seq', 'grp')
All inputs are finite; a program needn't handle non-finite values.
Results may differ from a plain program's by a relative error of at most 0.0075.
Values may be sent and summed in bfloat16 or wider, within the bound.
No kernel may reach another device: no remote copies, remote signals or barrier semaphores. Data moves between devices by JAX's collectives and lax.ppermute only.
A program may use at most 64 MiB of HBM per device.

v0:
```python
from functools import partial
import jax
import jax.numpy as jnp
from jax import lax
from jax.sharding import PartitionSpec as P

SPAN = 256
EPS = 1e-05
HIGH = lax.Precision.HIGHEST


def from_behind(value, axis, steps):
    count = lax.axis_size(axis)
    leading, last = (max(0, -steps), min(count, count - steps))
    return lax.ppermute(value, axis, [(source, source + steps) for source in range(leading, last)])


def prefix(value, axis, combine, identity):
    length, place = (lax.axis_size(axis), lax.axis_index(axis))
    everything = jax.tree.map(lambda part: lax.all_gather(part, axis), value)
    start = jax.tree.map(
        lambda part, zero: jnp.broadcast_to(jnp.asarray(zero, part.dtype), part.shape),
        value,
        identity,
    )

    def step(k, before):
        reached = k < place
        new = combine(before, jax.tree.map(lambda part: part[k], everything))
        return jax.tree.map(lambda a, b: jnp.where(reached, a, b), new, before)

    return lax.fori_loop(0, length, step, start)


def conv_rows(before, current, weight):
    width = weight.shape[0]
    padded = jnp.concatenate([before, current], axis=0).astype(jnp.float32)
    length = current.shape[0]
    total = jnp.zeros(current.shape, jnp.float32)
    for offset in range(width):
        total = total + weight[offset].astype(jnp.float32) * padded[offset : offset + length]
    return jax.nn.silu(total).astype(jnp.bfloat16)


def span_step(rate, skip, state, inputs):
    xvals, bmat, cmat, delta = inputs
    logdec = -delta * rate[None, :]
    cumul = jnp.cumsum(logdec, axis=0)
    length = cumul.shape[0]
    scores = jnp.einsum("tn,sn->ts", cmat, bmat, preferred_element_type=jnp.float32)
    lower = jnp.arange(length)[:, None] >= jnp.arange(length)[None, :]
    diffs = cumul.T[:, :, None] - cumul.T[:, None, :]
    decay = jnp.exp(jnp.where(lower[None], diffs, -jnp.inf))
    mixer = (scores[None] * decay * delta.T[:, None, :]).astype(jnp.bfloat16)
    intra = jnp.einsum("hts,shp->thp", mixer, xvals, preferred_element_type=jnp.float32)
    inter = jnp.exp(cumul)[:, :, None] * jnp.einsum(
        "tn,hpn->thp", cmat.astype(jnp.float32), state, precision=HIGH
    )
    output = intra + inter + skip[None, :, None] * xvals.astype(jnp.float32)
    tail = jnp.exp(cumul[-1][None, :] - cumul) * delta
    weighted = (tail[:, :, None] * bmat.astype(jnp.float32)[:, None, :]).astype(jnp.bfloat16)
    update = jnp.einsum("shp,shn->hpn", xvals, weighted, preferred_element_type=jnp.float32)
    new_state = jnp.exp(cumul[-1])[:, None, None] * state + update
    return (new_state, output)


def body(
    tokens,
    norm_gain,
    inner_weight,
    state_weight,
    step_weight,
    step_bias,
    decay_rate,
    skip_scale,
    conv_inner,
    conv_state,
    out_gain,
    out_weight,
):
    tok_rows = tokens.shape[0]
    model_width = tokens.shape[1]
    wide = tokens.astype(jnp.float32)
    normed = (
        wide * lax.rsqrt(jnp.mean(wide * wide, axis=1, keepdims=True) + EPS) * norm_gain
    ).astype(jnp.bfloat16)
    piece = lax.all_gather(inner_weight, "seq", axis=2, tiled=True)
    count = piece.shape[2]
    flat = piece.reshape(piece.shape[0], 2 * count)
    result = jnp.dot(normed, flat, preferred_element_type=jnp.float32).astype(jnp.bfloat16)
    inner = result.reshape(tok_rows, 2, count)
    state_flat = state_weight.reshape(model_width, -1)
    state_pre = (
        jnp.dot(normed, state_flat, preferred_element_type=jnp.float32)
        .astype(jnp.bfloat16)
        .reshape(tok_rows, 2, -1)
    )
    delta = jax.nn.softplus(
        jnp.dot(normed, step_weight, preferred_element_type=jnp.float32) + step_bias
    )
    inner_values = inner[:, 0, :]
    width = conv_inner.shape[0]
    first_kept = tok_rows - width + 1
    before_values, before_state = from_behind(
        (inner_values[first_kept:], state_pre[first_kept:]), "seq", 1
    )
    values = conv_rows(before_values, inner_values, conv_inner)
    conv_out = conv_rows(before_state, state_pre, conv_state)
    heads_here = delta.shape[1]
    head_width = values.shape[1] // heads_here
    state_width = conv_out.shape[2]
    blocks = tok_rows // SPAN
    xs_blocks = values.reshape(blocks, SPAN, heads_here, head_width)
    b_blocks = conv_out[:, 0, :].reshape(blocks, SPAN, state_width)
    c_blocks = conv_out[:, 1, :].reshape(blocks, SPAN, state_width)
    d_blocks = delta.reshape(blocks, SPAN, heads_here)
    initial = jnp.zeros((heads_here, head_width, state_width), jnp.float32)
    final_state, outputs = lax.scan(
        partial(span_step, decay_rate, skip_scale),
        initial,
        (xs_blocks, b_blocks, c_blocks, d_blocks),
    )
    cumdev = jnp.cumsum(-delta * decay_rate[None, :], axis=0)
    totals = cumdev[-1]

    def combine(earlier, later):
        return (earlier[0] + later[0], jnp.exp(later[0])[:, None, None] * earlier[1] + later[1])

    scanned = prefix(
        (totals, final_state), "seq", combine, (jnp.zeros_like(totals), jnp.zeros_like(final_state))
    )
    incoming = scanned[1]
    cmat_wide = conv_out[:, 1, :].astype(jnp.float32)
    carried = jnp.exp(cumdev)[:, :, None] * jnp.einsum(
        "tn,hpn->thp", cmat_wide, incoming, precision=HIGH
    )
    mixed_heads = (outputs.reshape(tok_rows, heads_here, head_width) + carried).reshape(
        tok_rows, heads_here * head_width
    )
    gated = mixed_heads * jax.nn.silu(inner[:, 1, :].astype(jnp.float32))
    squares = lax.psum(jnp.sum(gated * gated, axis=1), "grp")
    row_scale = lax.rsqrt(squares / (lax.axis_size("grp") * gated.shape[1]) + EPS)
    scaled = (gated * out_gain).astype(jnp.bfloat16)
    summed = jnp.dot(
        lax.all_gather(scaled, "grp", axis=1, tiled=True),
        out_weight,
        preferred_element_type=jnp.float32,
    )
    return (summed * row_scale[:, None]).astype(jnp.bfloat16)


def solution(mesh):
    return jax.shard_map(
        body,
        mesh=mesh,
        in_specs=(
            P("seq", None),
            P(),
            P(None, None, ("grp", "seq")),
            P(),
            P(None, "grp"),
            P("grp"),
            P("grp"),
            P("grp"),
            P(None, "grp"),
            P(),
            P("grp"),
            P(None, "grp"),
        ),
        out_specs=P("seq", "grp"),
        check_vma=False,
    )
```

profile of v0, /device:TPU:0, one launch (start us, length us, event | category | flops | bytes accessed | tf_op | source)
XLA Modules:
  0.0 453.3 jit_solution(12982020083999643823)
XLA Ops:
  7.3 2.4 fusion.40
  10.8 4.9 %collective-permute-start.1 = (bf16[3,2,128]{2,0,1:T(4,128)(2,1)S(1)}, bf16[3,2,128]{2,0,1:T(4,128)(2,1)S(1)}, u32[]{:S(2)}, u32[]{:S(2)}) collective-permute-start(bf16[3,2,128]{2,0,1:T(4,128)(2,1)S(1)} %slice_bitcast_fusion.2), channel_id=1, source_target_pairs={{0,4},{4,8},{8,12},{12,16},{16,20},{20,24},{24,28},{1,5},{5,9},{9,... | collective-permute-start | bytes 4616 | tf_op jit(solution)/shard_map/ppermute | solution.py:15
  16.4 1.5 compare_select_fusion.1
  20.8 174.0 %all-gather.6.cloned.1.call-done = bf16[2560,2,1280]{0,2,1:T(8,128)(2,1)} async-done(((bf16[2560,2,160]{0,2,1:T(8,128)(2,1)}), bf16[2560,2,1280]{0,2,1:T(8,128)(2,1)}) %all-gather.6.cloned.1.call-update) | async-done | bytes 13107216 | tf_op jit(solution)/shard_map/all_gather | solution.py:87
  194.8 11.2 %convolution_convert_fusion = bf16[512,2560]{1,0:T(8,128)(2,1)} fusion(bf16[2560,2560]{0,1:T(8,128)(2,1)} %bitcast.199, bf16[512,2560]{1,0:T(8,128)(2,1)S(1)} %copy-done.6, f32[2560]{0:T(1024)S(1)} %copy-done.16, f32[512]{0:T(512)S(1)} %add_rsqrt_fusion.1), kind=kOutput, calls=%fused_computation.59 | convolution fusion | flops 6717440000 | bytes 18362368 | tf_op jit(solution)/shard_map/dot_general | solution.py:90
  206.0 3.0 copy.65
  209.1 2.6 collective-permute-start
  211.8 2.0 slice_convert_fusion
  213.8 4.0 collective-permute-done
  218.5 3.2 multiply_convert_fusion.8
  222.4 71.2 %while.27 = (s32[]{:T(128)}, f32[20,64,128]{2,1,0:T(8,128)S(1)}, f32[2,256,20,64]{1,0,3,2:T(2,128)}, f32[2,256,20]{1,0,2:T(2,128)S(1)}, f32[20]{0:T(128)S(1)}, /...) while((s32[]{:T(128)}, f32[20,64,128]{2,1,0:T(8,128)S(1)}, ...), condition=%wide.region_4.5_spmd.clone, body=%wide.region_1.4_spmd.clone.sunk | while | flops 782684224 | bytes 15246184 | solution.py:118
  225.2 1.5 fusion.101
  229.1 27.0 %dynamic_update_slice.6 = f32[2,256,20,64]{1,0,3,2:T(2,128)} dynamic-update-slice(f32[2,256,20,64]{1,0,3,2:T(2,128)} %get-tuple-element.384, f32[1,256,20,64]{1,0,3,2:T(1,128)S(1)} %copy.106, s32[]{:T(128)} %get-tuple-element.382, s32[]{:T(128)} %constant.66.clone.1..sunk, s32[]{:T(128)} %constant.66.clone.1..sunk, s32[]{:T(128)} %constant.66.clone.1..sunk) | dynamic-update-slice | bytes 2621444 | tf_op jit(solution)/shard_map/while/body/jit(dynamic_update_index_in_dim)/dynamic_update_slice | solution.py:118
  260.8 1.5 fusion.101
  264.7 27.0 %dynamic_update_slice.6 = f32[2,256,20,64]{1,0,3,2:T(2,128)} dynamic-update-slice(f32[2,256,20,64]{1,0,3,2:T(2,128)} %get-tuple-element.384, f32[1,256,20,64]{1,0,3,2:T(1,128)S(1)} %copy.106, s32[]{:T(128)} %get-tuple-element.382, s32[]{:T(128)} %constant.66.clone.1..sunk, s32[]{:T(128)} %constant.66.clone.1..sunk, s32[]{:T(128)} %constant.66.clone.1..sunk) | dynamic-update-slice | bytes 2621444 | tf_op jit(solution)/shard_map/while/body/jit(dynamic_update_index_in_dim)/dynamic_update_slice | solution.py:118
  297.2 21.1 %all-gather.1 = f32[8,1,20]{2,1,0:T(1,128)S(1)} all-gather(f32[1,1,20]{2,1,0:T(1,128)S(1)} %bitcast.198), channel_id=1, replica_groups=mesh['seq'=8,'grp'=4] {'seq'}, dimensions={0}, use_global_device_ids=true | all-gather | bytes 720 | tf_op jit(solution)/shard_map/all_gather | solution.py:20
  318.3 4.9 %reshape.128 = f32[512,20,64]{0,2,1:T(8,128)} reshape(f32[2,256,20,64]{1,0,3,2:T(2,128)} %get-tuple-element.147) | data formatting | bytes 5242880 | tf_op jit(solution)/shard_map/reshape | solution.py:137
  323.2 59.1 %all-gather.10.cloned.1.call-done = f32[160,64,128]{2,1,0:T(8,128)} async-done(((f32[20,64,128]{2,1,0:T(8,128)}), f32[160,64,128]{2,1,0:T(8,128)}) %all-gather.10.cloned.1.call-update) | async-done | bytes 5242896 | tf_op jit(solution)/shard_map/all_gather | solution.py:20
  382.3 10.2 %while.28 = (s32[]{:T(128)}, f32[20,64,128]{2,1,0:T(8,128)S(1)}, s32[]{:T(128)}, f32[8,20]{1,0:T(8,128)S(1)}, f32[8,20,64,128]{3,2,1,0:T(8,128)}, /*index=5*/s32[]{:T(128)}, s32[]{:T(128)}) while((s32[]{:T(128)}, f32[20,64,128]{2,1,0:T(8,128)S(1)}, s32[]{:T(128)}, f32[8,20]{1,0:T(8,128)S(1)}, f32[8,20,64,128]{3,2,1,0:T(8,128)}, ...), condition=%wide.region_8.9_spmd.clone, body=%wide.region_7.8_spmd.clone.sunk | while | flops 655364 | bytes 1966425 | solution.py:32
  392.5 3.9 multiply_reduce_fusion
  396.4 2.0 fusion.51
  398.4 5.7 %psum.7 = f32[512]{0:T(512)S(1)} all-reduce(f32[512]{0:T(512)S(1)} %get-tuple-element.278), channel_id=1, replica_groups=mesh['seq'=8,'grp'=4] {'grp'}, use_global_device_ids=true, to_apply=%region_10.11 | all-reduce | flops 512 | bytes 4096 | tf_op jit(solution)/shard_map/psum | solution.py:141
  404.1 33.1 %all-gather.8.cloned.1.call-done = bf16[512,5120]{0,1:T(8,128)(2,1)} async-done(((bf16[512,1280]{0,1:T(8,128)(2,1)}), bf16[512,5120]{0,1:T(8,128)(2,1)}) %all-gather.8.cloned.1.call-update) | async-done | bytes 5242896 | tf_op jit(solution)/shard_map/all_gather | solution.py:145
  437.2 9.6 %fusion.52 = bf16[512,640]{1,0:T(8,128)(2,1)} fusion(bf16[512,5120]{0,1:T(8,128)(2,1)} %all-gather.8.cloned.1.call-done, bf16[5120,640]{1,0:T(8,128)(2,1)} %param.27, f32[512]{0:T(512)S(1)} %add_rsqrt_fusion), kind=kOutput, calls=%fused_computation.80 | convolution fusion | flops 3356098560 | bytes 12453888 | tf_op jit(solution)/shard_map/dot_general | solution.py:144
  (138 shorter events, 34.1 us)
Async XLA Ops:
  6.5 9.9 %copy-start = (bf16[2560,20]{0,1:T(8,128)(2,1)S(1)}, bf16[2560,20]{0,1:T(8,128)(2,1)}, u32[]{:S(2)}) copy-start(bf16[2560,20]{0,1:T(8,128)(2,1)} %param.20) | copy-start | bytes 307204
  6.5 3.2 copy-start.6
  6.5 3.2 copy-start.16
  6.5 188.2 %all-gather.6.cloned.1.call-start = ((), (), s32[]{:S(2)}) async-start(), calls=%async_computation | async-start | bytes 14745600 | tf_op jit(solution)/shard_map/all_gather | solution.py:87
  7.3 375.0 %all-gather.10.cloned.1.call-start = ((), (), s32[]{:S(2)}) async-start(), calls=%async_computation.2 | async-start | bytes 5898240 | tf_op jit(solution)/shard_map/all_gather | solution.py:20
  7.3 2.5 copy-start.15
  9.8 5.9 %copy-start.14 = (bf16[4,2,128]{2,1,0:T(2,128)(2,1)S(1)}, bf16[4,2,128]{2,1,0:T(2,128)(2,1)}, u32[]{:S(2)}) copy-start(bf16[4,2,128]{2,1,0:T(2,128)(2,1)} %param.25) | copy-start | bytes 6148
  9.8 6.6 %copy-start.17 = (f32[20]{0:T(128)S(1)}, f32[20]{0:T(128)}, u32[]{:S(2)}) copy-start(f32[20]{0:T(128)} %param.21) | copy-start | bytes 244
  10.8 7.3 %collective-permute-start.1 = (bf16[3,2,128]{2,0,1:T(4,128)(2,1)S(1)}, bf16[3,2,128]{2,0,1:T(4,128)(2,1)S(1)}, u32[]{:S(2)}, u32[]{:S(2)}) collective-permute-start(bf16[3,2,128]{2,0,1:T(4,128)(2,1)S(1)} %slice_bitcast_fusion.2), channel_id=1, source_target_pairs={{0,4},{4,8},{8,12},{12,16},{16,20},{20,24},{24,28},{1,5},{5,9},{9,... | collective-permute-start | bytes 4616 | tf_op jit(solution)/shard_map/ppermute | solution.py:15
  15.7 2.3 copy-start.10
  19.5 0.7 copy-start.7
  209.0 4.8 %copy-start.3 = (bf16[512,2560]{0,1:T(8,128)(2,1)}, bf16[512,2560]{0,1:T(8,128)(2,1)S(1)}, u32[]{:S(2)}) copy-start(bf16[512,2560]{0,1:T(8,128)(2,1)S(1)} %copy.65) | copy-start | bytes 7864324
  209.1 8.7 %collective-permute-start = (bf16[3,1280]{0,1:T(8,128)(2,1)S(1)}, bf16[3,1280]{0,1:T(8,128)(2,1)S(1)}, u32[]{:S(2)}, u32[]{:S(2)}) collective-permute-start(bf16[3,1280]{0,1:T(8,128)(2,1)S(1)} %slice_bitcast_fusion.1), channel_id=1, source_target_pairs={{0,4},{4,8},{8,12},{12,16},{16,20},{20,24},{24,28},{1,5},{5,9},{9,... | collective-permute-start | bytes 23048 | tf_op jit(solution)/shard_map/ppermute | solution.py:15
  221.8 0.7 copy-start.11
  221.8 0.7 copy-start.12
  229.1 28.9 %copy-start.9 = (f32[2,256,20]{1,0,2:T(2,128)S(1)}, f32[2,256,20]{1,0,2:T(2,128)}, u32[]{:S(2)}) copy-start(f32[2,256,20]{1,0,2:T(2,128)} %copy-done.8) | copy-start | bytes 122884 | tf_op jit(solution)/shard_map/while
  258.0 0.6 copy-start.8
  264.7 28.9 %copy-start.9 = (f32[2,256,20]{1,0,2:T(2,128)S(1)}, f32[2,256,20]{1,0,2:T(2,128)}, u32[]{:S(2)}) copy-start(f32[2,256,20]{1,0,2:T(2,128)} %copy-done.8) | copy-start | bytes 122884 | tf_op jit(solution)/shard_map/while
  293.6 0.8 copy-start.2
  294.5 142.7 %all-gather.8.cloned.1.call-start = ((), (), s32[]{:S(2)}) async-start(), calls=%async_computation.1 | async-start | bytes 6553600 | tf_op jit(solution)/shard_map/all_gather | solution.py:145
  318.3 74.2 %copy-start.5 = (f32[512,1,1280]{0,2,1:T(8,128)S(1)}, f32[512,1,1280]{0,2,1:T(8,128)}, u32[]{:S(2)}) copy-start(f32[512,1,1280]{0,2,1:T(8,128)} %get-tuple-element.268) | copy-start | bytes 7864324
  392.4 4.0 copy-start.4
  392.4 4.0 copy-start.13
  437.2 9.6 %copy-start.1 = (bf16[2560,20]{0,1:T(8,128)(2,1)S(1)}, bf16[2560,20]{0,1:T(8,128)(2,1)}, u32[]{:S(2)}) copy-start(bf16[2560,20]{0,1:T(8,128)(2,1)} %param.20) | copy-start | bytes 307204
  (1 other events, 0.6 us)
Sparse Core Ops, SparseCore 0:
  9.5 185.2 all-gather.5
  294.6 87.5 all-gather.9
  398.5 38.5 all-gather.7
where the time goes:
time: 458 us; the launch traced here: 453 us
  waiting for transfers between devices  271 us (59%)
  local copies, waits for them, and re-layouts  71 us (16%)
  matrix products  35.7 us (8%)
  other arithmetic  27.3 us (6%)
  blocking collectives  26.8 us (6%)
  between operations  13.5 us (3%)
  starting transfers between devices  7.63 us (2%)
    all_gather x1, waiting for transfers between devices, body(): piece = lax.all_gather(inner_weight, 'seq', axis=2, tiled=True)  174 us
    all_gather x1, waiting for transfers between devices, prefix(): everything = jax.tree.map(lambda part: lax.all_gather(part, axis), value)  59.1 us
    dynamic_update_slice x4, local copies, waits for them, and re-layouts, body(): lax.scan(partial(span_step, decay_rate, skip_scale), initial, (xs_blocks,...  56.8 us
    all_gather x1, waiting for transfers between devices, body(): lax.all_gather(scaled, 'grp', axis=1, tiled=True)  33.1 us
    all_gather x1, blocking collectives, prefix(): everything = jax.tree.map(lambda part: lax.all_gather(part, axis), value)  21.1 us
    dot_general x1, matrix products, body(): jnp.dot(normed, flat, preferred_element_type=jnp.float32)  11.2 us
    select_n x8, other arithmetic, step(): return jax.tree.map(lambda a, b: jnp.where(reached, a, b), new, before)  9.86 us
    dot_general x1, matrix products, body(): jnp.dot(lax.all_gather(scaled, 'grp', axis=1, tiled=True), out_weight, pr...  9.57 us
  transfers between devices with their start and end apart: 5, of which 4 were waited for; matrix products, arithmetic and copies ran while one was open for 4% of the time, Pallas kernels for 0%

commit v1 on v0

--- a/solution.py
+++ b/solution.py
@@ -1,3 +1,4 @@
+import functools
 from functools import partial
 import jax
 import jax.numpy as jnp
@@ -7,6 +8,24 @@
 SPAN = 256
 EPS = 1e-05
 HIGH = lax.Precision.HIGHEST
+
+
+def do_slices(local_block, named_axis):
+    how_many = lax.axis_size(named_axis)
+    parts_seen = [local_block]
+    for rr in range(1, how_many):
+        parts_seen.append(
+            lax.ppermute(
+                parts_seen[rr - 1],
+                named_axis,
+                perm=[(at, (at - 1) % how_many) for at in range(how_many)],
+            )
+        )
+    block_last = jnp.concatenate(parts_seen, axis=1)
+    return jnp.roll(block_last, lax.axis_index(named_axis) * local_block.shape[1], axis=1)
+
+
+match_digits_up = functools.partial(do_slices, named_axis="grp")
 
 
 def from_behind(value, axis, steps):
@@ -141,11 +160,7 @@
     squares = lax.psum(jnp.sum(gated * gated, axis=1), "grp")
     row_scale = lax.rsqrt(squares / (lax.axis_size("grp") * gated.shape[1]) + EPS)
     scaled = (gated * out_gain).astype(jnp.bfloat16)
-    summed = jnp.dot(
-        lax.all_gather(scaled, "grp", axis=1, tiled=True),
-        out_weight,
-        preferred_element_type=jnp.float32,
-    )
+    summed = jnp.dot(match_digits_up(scaled), out_weight, preferred_element_type=jnp.float32)
     return (summed * row_scale[:, None]).astype(jnp.bfloat16)
 
 

time: 458 us -> 481 us (1.050)
  blocking collectives: 26.8 us -> 39.6 us
  local copies, waits for them, and re-layouts: 71 us -> 82.1 us
    all_gather x1 -> x0, waiting for transfers between devices: 33.1 us -> none  [body(): lax.all_gather(scaled, 'grp', axis=1, tiled=True)]
    ppermute x0 -> x3, waiting for transfers between devices: none -> 30.3 us  [do_slices(): lax.ppermute(parts_seen[rr - 1], named_axis, perm=[(at, (at - 1) % how_ma...]
    psum x1, blocking collectives: 5.67 us -> 18.5 us  [body(): squares = lax.psum(jnp.sum(gated * gated, axis=1), 'grp')]
    unnamed x35 -> x49, local copies, waits for them, and re-layouts: 1.91 us -> 10.5 us
  transfers between devices with their start and end apart: 5 -> 7, of which waited for: 4 -> 5; matrix products, arithmetic and copies ran while one was open for 4% -> 4% of each run, Pallas kernels for 0% -> 0%
where the time goes in v1:
time: 481 us; the launch traced here: 477 us
  waiting for transfers between devices  268 us (56%)
  local copies, waits for them, and re-layouts  82.1 us (17%)
  blocking collectives  39.6 us (8%)
  matrix products  33.9 us (7%)
  other arithmetic  27.2 us (6%)
  between operations  13.8 us (3%)
  starting transfers between devices  11.4 us (2%)
    all_gather x1, waiting for transfers between devices, body(): piece = lax.all_gather(inner_weight, 'seq', axis=2, tiled=True)  174 us
    all_gather x1, waiting for transfers between devices, prefix(): everything = jax.tree.map(lambda part: lax.all_gather(part, axis), value)  59.1 us
    dynamic_update_slice x4, local copies, waits for them, and re-layouts, body(): lax.scan(partial(span_step, decay_rate, skip_scale), initial, (xs_blocks,...  56.8 us
    ppermute x3, waiting for transfers between devices, do_slices(): lax.ppermute(parts_seen[rr - 1], named_axis, perm=[(at, (at - 1) % how_ma...  30.3 us
    all_gather x1, blocking collectives, prefix(): everything = jax.tree.map(lambda part: lax.all_gather(part, axis), value)  21.1 us
    psum x1, blocking collectives, body(): squares = lax.psum(jnp.sum(gated * gated, axis=1), 'grp')  18.5 us
    dot_general x1, matrix products, body(): jnp.dot(normed, flat, preferred_element_type=jnp.float32)  11.2 us
    unnamed x49, local copies, waits for them, and re-layouts  10.5 us
  transfers between devices with their start and end apart: 7, of which 5 were waited for; matrix products, arithmetic and copies ran while one was open for 4% of the time, Pallas kernels for 0%

profile of v1, /device:TPU:0, one launch (start us, length us, event | category | flops | bytes accessed | tf_op | source)
XLA Modules:
  0.0 476.5 jit_solution(15878481144771462428)
XLA Ops:
  7.3 2.4 fusion.40
  10.8 4.9 %collective-permute-start.1 = (bf16[3,2,128]{2,0,1:T(4,128)(2,1)S(1)}, bf16[3,2,128]{2,0,1:T(4,128)(2,1)S(1)}, u32[]{:S(2)}, u32[]{:S(2)}) collective-permute-start(bf16[3,2,128]{2,0,1:T(4,128)(2,1)S(1)} %slice_bitcast_fusion.2), channel_id=1, source_target_pairs={{0,4},{4,8},{8,12},{12,16},{16,20},{20,24},{24,28},{1,5},{5,9},{9,... | collective-permute-start | bytes 4616 | tf_op jit(solution)/shard_map/ppermute | solution.py:34
  20.8 173.9 %all-gather.5.cloned.1.call-done = bf16[2560,2,1280]{0,2,1:T(8,128)(2,1)} async-done(((bf16[2560,2,160]{0,2,1:T(8,128)(2,1)}), bf16[2560,2,1280]{0,2,1:T(8,128)(2,1)}) %all-gather.5.cloned.1.call-update) | async-done | bytes 13107216 | tf_op jit(solution)/shard_map/all_gather | solution.py:106
  194.8 11.2 %convolution_convert_fusion = bf16[512,2560]{1,0:T(8,128)(2,1)} fusion(bf16[2560,2560]{0,1:T(8,128)(2,1)} %bitcast.198, bf16[512,2560]{1,0:T(8,128)(2,1)S(1)} %copy-done.8, f32[2560]{0:T(1024)S(1)} %copy-done.18, f32[512]{0:T(512)S(1)} %add_rsqrt_fusion.1), kind=kOutput, calls=%fused_computation.61 | convolution fusion | flops 6717440000 | bytes 18362368 | tf_op jit(solution)/shard_map/dot_general | solution.py:109
  206.0 3.0 copy.65
  209.2 2.6 collective-permute-start
  211.8 2.0 slice_convert_fusion
  213.9 4.0 collective-permute-done
  218.6 3.2 multiply_convert_fusion.8
  222.5 71.1 %while.27 = (s32[]{:T(128)}, f32[20,64,128]{2,1,0:T(8,128)S(1)}, f32[2,256,20,64]{1,0,3,2:T(2,128)}, f32[2,256,20]{1,0,2:T(2,128)S(1)}, f32[20]{0:T(128)S(1)}, /...) while((s32[]{:T(128)}, f32[20,64,128]{2,1,0:T(8,128)S(1)}, ...), condition=%wide.region_4.5_spmd.clone, body=%wide.region_1.4_spmd.clone.sunk | while | flops 782684224 | bytes 15246703 | solution.py:137
  231.0 27.1 %dynamic_update_slice.6 = f32[2,256,20,64]{1,0,3,2:T(2,128)} dynamic-update-slice(f32[2,256,20,64]{1,0,3,2:T(2,128)} %get-tuple-element.386, f32[1,256,20,64]{1,0,3,2:T(1,128)S(1)} %copy.106, s32[]{:T(128)S(6)} %copy.111, s32[]{:T(128)} %constant.85.clone.1..sunk, s32[]{:T(128)} %constant.85.clone.1..sunk, s32[]{:T(128)} %constant.85.clone.1..sunk) | dynamic-update-slice | bytes 2621444 | tf_op jit(solution)/shard_map/while/body/jit(dynamic_update_index_in_dim)/dynamic_update_slice | solution.py:137
  266.6 27.1 %dynamic_update_slice.6 = f32[2,256,20,64]{1,0,3,2:T(2,128)} dynamic-update-slice(f32[2,256,20,64]{1,0,3,2:T(2,128)} %get-tuple-element.386, f32[1,256,20,64]{1,0,3,2:T(1,128)S(1)} %copy.106, s32[]{:T(128)S(6)} %copy.111, s32[]{:T(128)} %constant.85.clone.1..sunk, s32[]{:T(128)} %constant.85.clone.1..sunk, s32[]{:T(128)} %constant.85.clone.1..sunk) | dynamic-update-slice | bytes 2621444 | tf_op jit(solution)/shard_map/while/body/jit(dynamic_update_index_in_dim)/dynamic_update_slice | solution.py:137
  297.1 21.1 %all-gather.1 = f32[8,1,20]{2,1,0:T(1,128)S(1)} all-gather(f32[1,1,20]{2,1,0:T(1,128)S(1)} %bitcast.197), channel_id=1, replica_groups=mesh['seq'=8,'grp'=4] {'seq'}, dimensions={0}, use_global_device_ids=true | all-gather | bytes 720 | tf_op jit(solution)/shard_map/all_gather | solution.py:39
  318.2 4.9 %reshape.128 = f32[512,20,64]{0,2,1:T(8,128)} reshape(f32[2,256,20,64]{1,0,3,2:T(2,128)} %get-tuple-element.147) | data formatting | bytes 5242880 | tf_op jit(solution)/shard_map/reshape | solution.py:156
  323.2 59.1 %all-gather.7.cloned.1.call-done = f32[160,64,128]{2,1,0:T(8,128)} async-done(((f32[20,64,128]{2,1,0:T(8,128)}), f32[160,64,128]{2,1,0:T(8,128)}) %all-gather.7.cloned.1.call-update) | async-done | bytes 5242896 | tf_op jit(solution)/shard_map/all_gather | solution.py:39
  382.3 10.2 %while.28 = (s32[]{:T(128)}, f32[20,64,128]{2,1,0:T(8,128)S(1)}, s32[]{:T(128)}, f32[8,20]{1,0:T(8,128)S(1)}, f32[8,20,64,128]{3,2,1,0:T(8,128)}, /*index=5*/s32[]{:T(128)}, s32[]{:T(128)}) while((s32[]{:T(128)}, f32[20,64,128]{2,1,0:T(8,128)S(1)}, s32[]{:T(128)}, f32[8,20]{1,0:T(8,128)S(1)}, f32[8,20,64,128]{3,2,1,0:T(8,128)}, ...), condition=%wide.region_8.9_spmd.clone, body=%wide.region_7.8_spmd.clone.sunk | while | flops 655364 | bytes 1966433 | solution.py:51
  392.5 3.9 multiply_reduce_fusion
  398.4 15.1 %collective-permute-done.2 = bf16[512,1280]{0,1:T(8,128)(2,1)S(1)} collective-permute-done((bf16[512,1280]{0,1:T(8,128)(2,1)S(1)}, bf16[512,1280]{0,1:T(8,128)(2,1)S(1)}, u32[]{:S(2)}, u32[]{:S(2)}) %collective-permute-start.2) | collective-permute-done | bytes 1310752 | tf_op jit(solution)/shard_map/ppermute | solution.py:18
  415.4 15.1 %collective-permute-done.3 = bf16[512,1280]{0,1:T(8,128)(2,1)S(1)} collective-permute-done((bf16[512,1280]{0,1:T(8,128)(2,1)S(1)}, bf16[512,1280]{0,1:T(8,128)(2,1)S(1)}, u32[]{:S(2)}, u32[]{:S(2)}) %collective-permute-start.3) | collective-permute-done | bytes 1310752 | tf_op jit(solution)/shard_map/ppermute | solution.py:18
  430.5 1.9 collective-permute-start.4
  432.4 18.5 %psum.7 = f32[512]{0:T(512)S(1)} all-reduce(f32[512]{0:T(512)S(1)} %get-tuple-element.280), channel_id=1, replica_groups=mesh['seq'=8,'grp'=4] {'grp'}, use_global_device_ids=true, to_apply=%region_10.11 | all-reduce | flops 512 | bytes 4096 | tf_op jit(solution)/shard_map/psum | solution.py:160
  453.3 2.6 constant_dynamic-update-slice_fusion.4
  459.5 2.5 constant_dynamic-update-slice_fusion
  462.0 7.7 %fusion.57 = bf16[512,640]{1,0:T(8,128)(2,1)} fusion(bf16[5120,640]{1,0:T(8,128)(2,1)S(1)} %bitcast.200, bf16[512,10240]{0,1:T(8,128)(2,1)} %constant_dynamic-update-slice_fusion, s32[]{:T(128)S(6)} %select_n.49, f32[512]{0:T(512)S(1)} %add_rsqrt_fusion), kind=kOutput, calls=%fused_computation.82 | convolution fusion | flops 3356098560 | bytes 12453892 | tf_op jit(solution)/shard_map/dot_general | solution.py:163
  (157 shorter events, 48.3 us)
Async XLA Ops:
  6.5 9.9 %copy-start = (bf16[2560,20]{0,1:T(8,128)(2,1)S(1)}, bf16[2560,20]{0,1:T(8,128)(2,1)}, u32[]{:S(2)}) copy-start(bf16[2560,20]{0,1:T(8,128)(2,1)} %param.20) | copy-start | bytes 307204
  6.5 3.2 copy-start.8
  6.5 3.2 copy-start.18
  6.5 188.2 %all-gather.5.cloned.1.call-start = ((), (), s32[]{:S(2)}) async-start(), calls=%async_computation | async-start | bytes 14745600 | tf_op jit(solution)/shard_map/all_gather | solution.py:106
  7.3 375.0 %all-gather.7.cloned.1.call-start = ((), (), s32[]{:S(2)}) async-start(), calls=%async_computation.1 | async-start | bytes 5898240 | tf_op jit(solution)/shard_map/all_gather | solution.py:39
  7.3 2.5 copy-start.17
  9.8 5.9 %copy-start.16 = (bf16[4,2,128]{2,1,0:T(2,128)(2,1)S(1)}, bf16[4,2,128]{2,1,0:T(2,128)(2,1)}, u32[]{:S(2)}) copy-start(bf16[4,2,128]{2,1,0:T(2,128)(2,1)} %param.25) | copy-start | bytes 6148
  9.8 6.6 %copy-start.19 = (f32[20]{0:T(128)S(1)}, f32[20]{0:T(128)}, u32[]{:S(2)}) copy-start(f32[20]{0:T(128)} %param.21) | copy-start | bytes 244
  10.8 7.3 %collective-permute-start.1 = (bf16[3,2,128]{2,0,1:T(4,128)(2,1)S(1)}, bf16[3,2,128]{2,0,1:T(4,128)(2,1)S(1)}, u32[]{:S(2)}, u32[]{:S(2)}) collective-permute-start(bf16[3,2,128]{2,0,1:T(4,128)(2,1)S(1)} %slice_bitcast_fusion.2), channel_id=1, source_target_pairs={{0,4},{4,8},{8,12},{12,16},{16,20},{20,24},{24,28},{1,5},{5,9},{9,... | collective-permute-start | bytes 4616 | tf_op jit(solution)/shard_map/ppermute | solution.py:34
  209.0 4.8 %copy-start.3 = (bf16[512,2560]{0,1:T(8,128)(2,1)}, bf16[512,2560]{0,1:T(8,128)(2,1)S(1)}, u32[]{:S(2)}) copy-start(bf16[512,2560]{0,1:T(8,128)(2,1)S(1)} %copy.65) | copy-start | bytes 7864324
  209.2 8.7 %collective-permute-start = (bf16[3,1280]{0,1:T(8,128)(2,1)S(1)}, bf16[3,1280]{0,1:T(8,128)(2,1)S(1)}, u32[]{:S(2)}, u32[]{:S(2)}) collective-permute-start(bf16[3,1280]{0,1:T(8,128)(2,1)S(1)} %slice_bitcast_fusion.1), channel_id=1, source_target_pairs={{0,4},{4,8},{8,12},{12,16},{16,20},{20,24},{24,28},{1,5},{5,9},{9,... | collective-permute-start | bytes 23048 | tf_op jit(solution)/shard_map/ppermute | solution.py:34
  230.0 28.1 %copy-start.11 = (f32[2,256,20]{1,0,2:T(2,128)S(1)}, f32[2,256,20]{1,0,2:T(2,128)}, u32[]{:S(2)}) copy-start(f32[2,256,20]{1,0,2:T(2,128)} %copy-done.10) | copy-start | bytes 122884 | tf_op jit(solution)/shard_map/while
  265.6 28.1 %copy-start.11 = (f32[2,256,20]{1,0,2:T(2,128)S(1)}, f32[2,256,20]{1,0,2:T(2,128)}, u32[]{:S(2)}) copy-start(f32[2,256,20]{1,0,2:T(2,128)} %copy-done.10) | copy-start | bytes 122884 | tf_op jit(solution)/shard_map/while
  318.2 74.2 %copy-start.7 = (f32[512,1,1280]{0,2,1:T(8,128)S(1)}, f32[512,1,1280]{0,2,1:T(8,128)}, u32[]{:S(2)}) copy-start(f32[512,1,1280]{0,2,1:T(8,128)} %get-tuple-element.268) | copy-start | bytes 7864324
  392.5 4.0 copy-start.4
  392.5 4.0 copy-start.15
  398.3 32.2 %copy-start.5 = (bf16[512,1280]{0,1:T(8,128)(2,1)}, bf16[512,1280]{0,1:T(8,128)(2,1)S(1)}, u32[]{:S(2)}) copy-start(bf16[512,1280]{0,1:T(8,128)(2,1)S(1)} %get-tuple-element.279) | copy-start | bytes 3932164
  398.3 15.1 %collective-permute-start.2 = (bf16[512,1280]{0,1:T(8,128)(2,1)S(1)}, bf16[512,1280]{0,1:T(8,128)(2,1)S(1)}, u32[]{:S(2)}, u32[]{:S(2)}) collective-permute-start(bf16[512,1280]{0,1:T(8,128)(2,1)S(1)} %get-tuple-element.279), channel_id=1, source_target_pairs={{0,3},{1,0},{2,1},{3,2},{4,7},{5,4},{6,5},{7,6},{8,11},{9,8},{10,9... | collective-permute-start | bytes 3932168 | tf_op jit(solution)/shard_map/ppermute | solution.py:18
  413.5 17.0 %collective-permute-start.3 = (bf16[512,1280]{0,1:T(8,128)(2,1)S(1)}, bf16[512,1280]{0,1:T(8,128)(2,1)S(1)}, u32[]{:S(2)}, u32[]{:S(2)}) collective-permute-start(bf16[512,1280]{0,1:T(8,128)(2,1)S(1)} %collective-permute-done.2), channel_id=1, source_target_pairs={{0,3},{1,0},{2,1},{3,2},{4,7},{5,4},{6,5},{7,6},{8,11},{9,8},{10,9... | collective-permute-start | bytes 3932168 | tf_op jit(solution)/shard_map/ppermute | solution.py:18
  430.5 22.8 %collective-permute-start.4 = (bf16[512,1280]{0,1:T(8,128)(2,1)S(1)}, bf16[512,1280]{0,1:T(8,128)(2,1)}, u32[]{:S(2)}, u32[]{:S(2)}) collective-permute-start(bf16[512,1280]{0,1:T(8,128)(2,1)S(1)} %collective-permute-done.3), channel_id=1, source_target_pairs={{0,3},{1,0},{2,1},{3,2},{4,7},{5,4},{6,5},{7,6},{8,11},{9,8},{10,9... | collective-permute-start | bytes 3932168 | tf_op jit(solution)/shard_map/ppermute | solution.py:18
  452.1 3.8 copy-start.6
  453.3 8.7 %slice-start = ((s8[6553600]{0:T(1024)(128)(4,1)}), s8[4194304]{0:T(1024)(128)(4,1)S(1)}, s32[]{:S(2)}) async-start(s8[6553600]{0:T(1024)(128)(4,1)} %bitcast.199), calls=%async_computation.2 | async-start | bytes 8388608
  457.1 4.8 %slice-start.1 = ((s8[6553600]{0:T(1024)(128)(4,1)}), s8[2359296]{0:T(1024)(128)(4,1)S(1)}, s32[]{:S(2)}) async-start(s8[6553600]{0:T(1024)(128)(4,1)} %bitcast.199), calls=%async_computation.3 | async-start | bytes 4718592
  462.0 7.7 %copy-start.1 = (bf16[2560,20]{0,1:T(8,128)(2,1)S(1)}, bf16[2560,20]{0,1:T(8,128)(2,1)}, u32[]{:S(2)}) copy-start(bf16[2560,20]{0,1:T(8,128)(2,1)} %param.20) | copy-start | bytes 307204
  (7 other events, 6.4 us)
Sparse Core Ops, SparseCore 0:
  9.5 185.2 all-gather.4
  294.6 87.6 all-gather.6
